TPU v7x, 32 devices: a whole 2x2x4 slice. The times are simulated.
32 devices in a mesh: dp: 8 (over y, x, core), vocab: 4 (over z).
Axes of the slice: x: 2, y: 2, z: 4, core: 2. Of those that a mesh axis runs over, the one named last changes fastest.
Arguments:
- hidden: float32 [16, 4608], P('dp'), may hold values from -6 to 6
- norm_gain: float32 [4608], replicated, may hold values from 0.5 to 1.5
- embed_table: bfloat16 [12288, 4608], P(('dp', 'vocab')), as said below
- tokens: int32 [16, 3], replicated, may hold values from 0 to 12287, as said below
Outputs:
- log_probs: float32 [16, 3], P('dp')
- final_hidden: float32 [16, 4608], P('dp')
Inputs may be any that keep to these rules, and one draw needn't show every extreme that they name: `tokens`: token ids are vocabulary entries. `embed_table`: entries lie between -21 / sqrt(4608) and 21 / sqrt(4608).
All inputs are finite; a program needn't handle non-finite values.
Results may differ from a plain program's by a relative error of at most 0.0003.
Values may be sent and summed in bfloat16 or wider, within the bound.
A program may use at most 64 MiB of HBM per device.

v0:
```python
import math
import jax
import jax.numpy as jnp
from jax import lax
from jax.sharding import PartitionSpec as P

D = 4608
STEPS = 3
epsilon_value = 1e-06
softcap_value = 30.0


def project_rows(normed, embed_table):
    return lax.dot_general(
        normed, embed_table, (((1,), (1,)), ((), ())), preferred_element_type=jnp.float32
    )


def on_device(hidden, norm_gain, embed_table, tokens):
    own_rows = hidden.shape[0]
    shard_rows = embed_table.shape[0]
    own_start = lax.axis_index("dp") * own_rows
    shard_start = (
        lax.axis_index("dp") * lax.axis_size("vocab") + lax.axis_index("vocab")
    ) * shard_rows
    scale_factor = math.sqrt(D)
    local_ids = jnp.transpose(tokens) - shard_start
    columns = lax.broadcasted_iota(jnp.int32, (1, 1, shard_rows), 2)
    matches = local_ids[:, :, None] == columns
    onehot = matches.astype(jnp.bfloat16)
    found = jnp.einsum("sbv,vd->sbd", onehot, embed_table, preferred_element_type=jnp.float32)
    current = hidden
    partial_value = lax.psum_scatter(
        found.astype(jnp.bfloat16), "dp", scatter_dimension=1, tiled=True
    )
    summed = lax.psum(partial_value, "vocab").astype(jnp.float32)
    results = []
    for decode_step in range(STEPS):
        square_mean = jnp.mean(current * current, axis=-1, keepdims=True)
        normed = (current * lax.rsqrt(square_mean + epsilon_value) * norm_gain).astype(jnp.bfloat16)
        logits = project_rows(lax.all_gather(normed, "dp", axis=0, tiled=True), embed_table)
        capped = softcap_value * jnp.tanh(logits / softcap_value)
        exp_total = jnp.sum(jnp.exp(capped), axis=-1)
        target = jnp.sum(jnp.where(matches[decode_step], capped, 0.0), axis=-1)
        exp_total, target = lax.psum((exp_total, target), ("dp", "vocab"))
        exp_total = lax.dynamic_slice_in_dim(exp_total, own_start, own_rows, 0)
        target = lax.dynamic_slice_in_dim(target, own_start, own_rows, 0)
        results.append(target - jnp.log(exp_total))
        current = current + scale_factor * summed[decode_step]
    return (jnp.stack(results, axis=1), current)


def solution(mesh):
    return jax.shard_map(
        on_device,
        mesh=mesh,
        in_specs=(P("dp", None), P(), P(("dp", "vocab"), None), P()),
        out_specs=(P("dp", None), P("dp", None)),
        check_vma=False,
    )
```

profile of v0, /device:TPU:12, one launch (start us, length us, event | category | flops | bytes accessed | tf_op | source)
XLA Modules:
  0.0 184.4 jit_solution(427541426465696467)
XLA Ops:
  7.2 0.8 subtract_bitcast_fusion
  8.1 1.1 copy-done
  9.2 1.5 convolution_convert_fusion
  12.0 0.7 iota_compare_fusion
  12.7 53.5 %all-reduce.4.cloned.1.call-done = bf16[3,16,4608]{2,1,0:T(8,128)(2,1)} async-done(((bf16[3,16,4608]{2,1,0:T(8,128)(2,1)}), bf16[3,16,4608]{2,1,0:T(8,128)(2,1)}) %all-reduce.4.cloned.1.call-update) | async-done | bytes 442384
  66.2 1.6 constant_dynamic-slice_fusion
  67.8 17.1 %psum.51 = bf16[3,2,4608]{2,1,0:T(2,128)(2,1)} all-reduce(bf16[3,2,4608]{2,1,0:T(2,128)(2,1)} %constant_dynamic-slice_fusion), channel_id=1, replica_groups=mesh['dp'=8,'vocab'=4] {'vocab'}, use_global_device_ids=true, to_apply=%region_6.7 | all-reduce | flops 27648 | bytes 110592 | tf_op jit(solution)/shard_map/psum | solution.py:36
  85.0 0.9 convert_element_type.18
  85.8 1.6 fusion.8
  87.6 1.5 fusion.14
  89.1 9.8 %all-gather.2 = bf16[8,2,4608]{2,1,0:T(2,128)(2,1)} all-gather(bf16[1,2,4608]{2,1,0:T(2,128)(2,1)S(1)} %get-tuple-element.27), channel_id=1, replica_groups=mesh['dp'=8,'vocab'=4] {'dp'}, dimensions={0}, use_global_device_ids=true | all-gather | bytes 165888 | tf_op jit(solution)/shard_map/all_gather | solution.py:41
  99.0 1.6 reshape.41
  100.6 2.6 %fusion.2 = f32[16,384]{1,0:T(8,128)} fusion(bf16[16,4608]{1,0:T(8,128)(2,1)} %reshape.41, bf16[384,4608]{1,0:T(8,128)(2,1)S(1)} %copy-done), kind=kOutput, calls=%fused_computation.4 | convolution fusion | flops 56635392 | bytes 3710976 | tf_op jit(solution)/shard_map/dot_general | solution.py:14
  103.2 9.6 %all-gather.1 = bf16[8,2,4608]{2,1,0:T(2,128)(2,1)} all-gather(bf16[1,2,4608]{2,1,0:T(2,128)(2,1)S(1)} %copy-done.2), channel_id=1, replica_groups=mesh['dp'=8,'vocab'=4] {'dp'}, dimensions={0}, use_global_device_ids=true | all-gather | bytes 165888 | tf_op jit(solution)/shard_map/all_gather | solution.py:41
  112.8 1.6 reshape.39
  114.4 2.6 %fusion.4 = f32[16,384]{1,0:T(8,128)} fusion(bf16[16,4608]{1,0:T(8,128)(2,1)} %reshape.39, bf16[384,4608]{1,0:T(8,128)(2,1)S(1)} %copy-done), kind=kOutput, calls=%fused_computation.7 | convolution fusion | flops 56635392 | bytes 3710976 | tf_op jit(solution)/shard_map/dot_general | solution.py:14
  117.0 9.8 %all-gather = bf16[8,2,4608]{2,1,0:T(2,128)(2,1)} all-gather(bf16[1,2,4608]{2,1,0:T(2,128)(2,1)S(1)} %copy-done.1), channel_id=1, replica_groups=mesh['dp'=8,'vocab'=4] {'dp'}, dimensions={0}, use_global_device_ids=true | all-gather | bytes 165888 | tf_op jit(solution)/shard_map/all_gather | solution.py:41
  126.8 1.6 reshape.37
  128.4 2.8 %select_reduce_fusion.2 = (f32[16]{0:T(128)S(1)}, f32[16]{0:T(128)S(1)}, f32[16]{0:T(128)S(1)}, f32[16]{0:T(128)S(1)}, f32[16]{0:T(128)}, /*index=5*/f32[16]{0:T(128)}) fusion(pred[3,16,384]{2,1,0:T(8,128)(4,1)} %iota_compare_fusion, f32[16,384]{1,0:T(8,128)} %fusion.2, f32[16,384]{1,0:T(8,128)} %fusion.4, bf16[16,4608]{1,0:T(8,128)(2,1)} %reshape.37, ...), kind=kOutput, calls=%fused_computation.32 | convolution fusion | flops 56690592 | bytes 3754368 | tf_op jit(solution)/shard_map/dot_general | solution.py:14
  131.2 43.4 %all-reduce.1 = (f32[16]{0:T(128)}, f32[16]{0:T(128)}, f32[16]{0:T(128)}, f32[16]{0:T(128)}, f32[16]{0:T(128)}, /*index=5*/f32[16]{0:T(128)}) all-reduce(f32[16]{0:T(128)S(1)} %get-tuple-element.12, f32[16]{0:T(128)S(1)} %get-tuple-element.13, f32[16]{0:T(128)} %get-tuple-element.14, ...), channel_id=1, replica_groups=mesh['dp'=8,'vocab'=4] {'dp','vocab'}, use_global_device_ids=true, to_apply=%region_16.17 | all-reduce | flops 96 | bytes 768 | tf_op jit(solution)/shard_map/psum | solution.py:45
  174.7 0.7 subtract_bitcast_fusion.3
  175.4 0.7 subtract_bitcast_fusion.2
  176.1 0.8 subtract_bitcast_fusion.1
  176.9 0.7 copy.7
  (15 shorter events, 0.9 us)
Async XLA Ops:
  7.2 2.0 %copy-start = (bf16[384,4608]{1,0:T(8,128)(2,1)S(1)}, bf16[384,4608]{1,0:T(8,128)(2,1)}, u32[]{:S(2)}) copy-start(bf16[384,4608]{1,0:T(8,128)(2,1)} %param.6) | copy-start | bytes 10616836
  7.2 3.6 %copy-start.3 = (u32[32]{0:T(128)S(1)}, u32[32]{0:T(128)}, u32[]{:S(2)}) copy-start(u32[32]{0:T(128)} %constant.39) | copy-start | bytes 388
  7.2 59.0 %all-reduce.4.cloned.1.call-start = ((), (), s32[]{:S(2)}) async-start(), calls=%async_computation | async-start | bytes 884736
  100.6 2.6 %copy-start.2 = (bf16[1,2,4608]{2,1,0:T(2,128)(2,1)S(1)}, bf16[1,2,4608]{2,1,0:T(2,128)(2,1)}, u32[]{:S(2)}) copy-start(bf16[1,2,4608]{2,1,0:T(2,128)(2,1)} %get-tuple-element.26) | copy-start | bytes 55300
  114.4 2.6 %copy-start.1 = (bf16[1,2,4608]{2,1,0:T(2,128)(2,1)S(1)}, bf16[1,2,4608]{2,1,0:T(2,128)(2,1)}, u32[]{:S(2)}) copy-start(bf16[1,2,4608]{2,1,0:T(2,128)(2,1)} %get-tuple-element.28) | copy-start | bytes 55300
Sparse Core Ops, SparseCore 0:
  11.1 55.0 all-reduce.3
where the time goes:
time: 185 us; the launch traced here: 184 us
  blocking collectives  89.8 us (49%)
  waiting for transfers between devices  53.6 us (29%)
  between operations  14.8 us (8%)
  matrix products  9.52 us (5%)
  local copies, waits for them, and re-layouts  8.82 us (5%)
  other arithmetic  7.92 us (4%)
    unnamed x2, waiting for transfers between devices  53.6 us
    psum x1, blocking collectives, on_device(): exp_total, target = lax.psum((exp_total, target), ('dp', 'vocab'))  43.4 us
    all_gather x3, blocking collectives, on_device(): lax.all_gather(normed, 'dp', axis=0, tiled=True)  29.2 us
    psum x1, blocking collectives, on_device(): summed = lax.psum(partial_value, 'vocab').astype(jnp.float32)  17.1 us
    unnamed x14, local copies, waits for them, and re-layouts  8.82 us
    dot_general x3, matrix products, project_rows(): lax.dot_general(normed, embed_table, (((1,), (1,)), ((), ())), preferred_...  7.99 us
  transfers between devices with their start and end apart: 1, of which 1 were waited for; matrix products, arithmetic and copies ran while one was open for 1% of the time, Pallas kernels for 0%

commit v1 on v0

--- a/solution.py
+++ b/solution.py
@@ -42,7 +42,7 @@
         capped = softcap_value * jnp.tanh(logits / softcap_value)
         exp_total = jnp.sum(jnp.exp(capped), axis=-1)
         target = jnp.sum(jnp.where(matches[decode_step], capped, 0.0), axis=-1)
-        exp_total, target = lax.psum((exp_total, target), ("dp", "vocab"))
+        exp_total, target = lax.psum(lax.psum((exp_total, target), "vocab"), "dp")
         exp_total = lax.dynamic_slice_in_dim(exp_total, own_start, own_rows, 0)
         target = lax.dynamic_slice_in_dim(target, own_start, own_rows, 0)
         results.append(target - jnp.log(exp_total))

time: 185 us -> 167 us (0.903)
  blocking collectives: 89.8 us -> 71.9 us
    psum x1 -> x2, blocking collectives: 43.4 us -> 25.5 us  [on_device(): exp_total, target = lax.psum(lax.psum((exp_total, target), 'vocab'), 'dp')]
where the time goes in v1:
time: 167 us; the launch traced here: 165 us
  blocking collectives  71.9 us (43%)
  waiting for transfers between devices  53.6 us (32%)
  between operations  14.8 us (9%)
  matrix products  9.52 us (6%)
  local copies, waits for them, and re-layouts  8.83 us (5%)
  other arithmetic  6.52 us (4%)
    unnamed x2, waiting for transfers between devices  53.6 us
    all_gather x3, blocking collectives, on_device(): lax.all_gather(normed, 'dp', axis=0, tiled=True)  29.2 us
    psum x2, blocking collectives, on_device(): exp_total, target = lax.psum(lax.psum((exp_total, target), 'vocab'), 'dp')  25.5 us
    psum x1, blocking collectives, on_device(): summed = lax.psum(partial_value, 'vocab').astype(jnp.float32)  17.1 us
    unnamed x14, local copies, waits for them, and re-layouts  8.83 us
    dot_general x3, matrix products, project_rows(): lax.dot_general(normed, embed_table, (((1,), (1,)), ((), ())), preferred_...  7.99 us
  transfers between devices with their start and end apart: 1, of which 1 were waited for; matrix products, arithmetic and copies ran while one was open for 1% of the time, Pallas kernels for 0%

profile of v1, /device:TPU:12, one launch (start us, length us, event | category | flops | bytes accessed | tf_op | source)
XLA Modules:
  0.0 165.1 jit_solution(7500615834331544840)
XLA Ops:
  7.2 0.8 subtract_bitcast_fusion
  8.1 1.1 copy-done
  9.2 1.5 convolution_convert_fusion
  10.8 0.6 dynamic-slice
  12.0 0.7 iota_compare_fusion
  12.7 53.5 %all-reduce.5.cloned.1.call-done = bf16[3,16,4608]{2,1,0:T(8,128)(2,1)} async-done(((bf16[3,16,4608]{2,1,0:T(8,128)(2,1)}), bf16[3,16,4608]{2,1,0:T(8,128)(2,1)}) %all-reduce.5.cloned.1.call-update) | async-done | bytes 442384
  66.2 1.6 constant_dynamic-slice_fusion
  67.8 17.1 %psum.95 = bf16[3,2,4608]{2,1,0:T(2,128)(2,1)} all-reduce(bf16[3,2,4608]{2,1,0:T(2,128)(2,1)} %constant_dynamic-slice_fusion), channel_id=1, replica_groups=mesh['dp'=8,'vocab'=4] {'vocab'}, use_global_device_ids=true, to_apply=%region_8.9 | all-reduce | flops 27648 | bytes 110592 | tf_op jit(solution)/shard_map/psum | solution.py:36
  85.0 0.9 convert_element_type.18
  85.8 1.6 fusion.8
  87.6 1.5 fusion.14
  89.1 9.8 %all-gather.2 = bf16[8,2,4608]{2,1,0:T(2,128)(2,1)} all-gather(bf16[1,2,4608]{2,1,0:T(2,128)(2,1)S(1)} %get-tuple-element.33), channel_id=1, replica_groups=mesh['dp'=8,'vocab'=4] {'dp'}, dimensions={0}, use_global_device_ids=true | all-gather | bytes 165888 | tf_op jit(solution)/shard_map/all_gather | solution.py:41
  99.0 1.6 reshape.41
  100.6 2.6 %fusion.2 = f32[16,384]{1,0:T(8,128)} fusion(bf16[16,4608]{1,0:T(8,128)(2,1)} %reshape.41, bf16[384,4608]{1,0:T(8,128)(2,1)S(1)} %copy-done), kind=kOutput, calls=%fused_computation.4 | convolution fusion | flops 56635392 | bytes 3710976 | tf_op jit(solution)/shard_map/dot_general | solution.py:14
  103.2 9.6 %all-gather.1 = bf16[8,2,4608]{2,1,0:T(2,128)(2,1)} all-gather(bf16[1,2,4608]{2,1,0:T(2,128)(2,1)S(1)} %copy-done.2), channel_id=1, replica_groups=mesh['dp'=8,'vocab'=4] {'dp'}, dimensions={0}, use_global_device_ids=true | all-gather | bytes 165888 | tf_op jit(solution)/shard_map/all_gather | solution.py:41
  112.8 1.6 reshape.39
  114.4 2.6 %fusion.4 = f32[16,384]{1,0:T(8,128)} fusion(bf16[16,4608]{1,0:T(8,128)(2,1)} %reshape.39, bf16[384,4608]{1,0:T(8,128)(2,1)S(1)} %copy-done), kind=kOutput, calls=%fused_computation.7 | convolution fusion | flops 56635392 | bytes 3710976 | tf_op jit(solution)/shard_map/dot_general | solution.py:14
  117.0 9.8 %all-gather = bf16[8,2,4608]{2,1,0:T(2,128)(2,1)} all-gather(bf16[1,2,4608]{2,1,0:T(2,128)(2,1)S(1)} %copy-done.1), channel_id=1, replica_groups=mesh['dp'=8,'vocab'=4] {'dp'}, dimensions={0}, use_global_device_ids=true | all-gather | bytes 165888 | tf_op jit(solution)/shard_map/all_gather | solution.py:41
  126.8 1.6 reshape.37
  128.4 2.8 %select_reduce_fusion.2 = (f32[16]{0:T(128)S(1)}, f32[16]{0:T(128)S(1)}, f32[16]{0:T(128)S(1)}, f32[16]{0:T(128)S(1)}, f32[16]{0:T(128)}, /*index=5*/f32[16]{0:T(128)}) fusion(pred[3,16,384]{2,1,0:T(8,128)(4,1)} %iota_compare_fusion, f32[16,384]{1,0:T(8,128)} %fusion.2, f32[16,384]{1,0:T(8,128)} %fusion.4, bf16[16,4608]{1,0:T(8,128)(2,1)} %reshape.37, ...), kind=kOutput, calls=%fused_computation.32 | convolution fusion | flops 56690592 | bytes 3754368 | tf_op jit(solution)/shard_map/dot_general | solution.py:14
  131.2 13.1 %all-reduce.2 = (f32[16]{0:T(128)}, f32[16]{0:T(128)}, f32[16]{0:T(128)}, f32[16]{0:T(128)}, f32[16]{0:T(128)}, /*index=5*/f32[16]{0:T(128)}) all-reduce(f32[16]{0:T(128)S(1)} %get-tuple-element.12, f32[16]{0:T(128)S(1)} %get-tuple-element.13, f32[16]{0:T(128)} %get-tuple-element.14, ...), channel_id=1, replica_groups=mesh['dp'=8,'vocab'=4] {'vocab'}, use_global_device_ids=true, to_apply=%region_21.22 | all-reduce | flops 96 | bytes 768 | tf_op jit(solution)/shard_map/psum | solution.py:45
  144.3 12.4 %all-reduce.1 = (f32[16]{0:T(128)S(1)}, f32[16]{0:T(128)S(1)}, f32[16]{0:T(128)S(1)}, f32[16]{0:T(128)S(1)}, f32[16]{0:T(128)}, /*index=5*/f32[16]{0:T(128)}) all-reduce(f32[16]{0:T(128)} %get-tuple-element.22, f32[16]{0:T(128)} %get-tuple-element.23, f32[16]{0:T(128)} %get-tuple-element.24, ...), channel_id=1, replica_groups=mesh['dp'=8,'vocab'=4] {'dp'}, use_global_device_ids=true, to_apply=%region_22.23 | all-reduce | flops 96 | bytes 768 | tf_op jit(solution)/shard_map/psum | solution.py:45
  156.8 0.7 subtract_bitcast_fusion.3
  157.6 0.7 copy.7
  (16 shorter events, 0.4 us)
Async XLA Ops:
  7.2 2.0 %copy-start = (bf16[384,4608]{1,0:T(8,128)(2,1)S(1)}, bf16[384,4608]{1,0:T(8,128)(2,1)}, u32[]{:S(2)}) copy-start(bf16[384,4608]{1,0:T(8,128)(2,1)} %param.6) | copy-start | bytes 10616836
  7.2 3.6 %copy-start.3 = (u32[32]{0:T(128)S(1)}, u32[32]{0:T(128)}, u32[]{:S(2)}) copy-start(u32[32]{0:T(128)} %constant.39) | copy-start | bytes 388
  7.2 59.0 %all-reduce.5.cloned.1.call-start = ((), (), s32[]{:S(2)}) async-start(), calls=%async_computation | async-start | bytes 884736
  100.6 2.6 %copy-start.2 = (bf16[1,2,4608]{2,1,0:T(2,128)(2,1)S(1)}, bf16[1,2,4608]{2,1,0:T(2,128)(2,1)}, u32[]{:S(2)}) copy-start(bf16[1,2,4608]{2,1,0:T(2,128)(2,1)} %get-tuple-element.32) | copy-start | bytes 55300
  114.4 2.6 %copy-start.1 = (bf16[1,2,4608]{2,1,0:T(2,128)(2,1)S(1)}, bf16[1,2,4608]{2,1,0:T(2,128)(2,1)}, u32[]{:S(2)}) copy-start(bf16[1,2,4608]{2,1,0:T(2,128)(2,1)} %get-tuple-element.34) | copy-start | bytes 55300
Sparse Core Ops, SparseCore 0:
  11.1 55.0 all-reduce.4
